TPU v7x, 32 devices: a whole 2x2x4 slice. The times are simulated.
32 devices in a mesh: groups: 2 (over y), section: 2 (over core), rank: 8 (over z, x).
Axes of the slice: x: 2, y: 2, z: 4, core: 2. Of those that a mesh axis runs over, the one named last changes fastest.
Arguments:
- rows_in: float32 [2, 16, 8192], P('section', ('groups', 'rank')), parts along dimension 1, may hold values from -54 to 54
- query: bfloat16 [2, 16, 8192], P('section', ('groups', 'rank')), parts along dimension 1, may hold values from -6 to 6
- key_cache: bfloat16 [2, 16, 256, 1024], P('section', ('groups', 'rank')), parts along dimension 1, may hold values from -6 to 6
- value_cache: bfloat16 [2, 16, 256, 1024], P('section', ('groups', 'rank')), parts along dimension 1, may hold values from -6 to 6
- key_new: bfloat16 [2, 16, 1024], P('section', ('groups', 'rank')), parts along dimension 1, may hold values from -6 to 6
- value_new: bfloat16 [2, 16, 1024], P('section', ('groups', 'rank')), parts along dimension 1, may hold values from -6 to 6
- lengths: int32 [2, 16], P('section', ('groups', 'rank')), parts along dimension 1, may hold values from 1 to 256, as said below
- norm_gain: float32 [2, 8192], P('section'), may hold values from 0.25 to 1.75
- w_up: bfloat16 [2, 8192, 14336], P('section', None, 'rank'), may hold values from -0.0625 to 0.0625
- w_down: bfloat16 [2, 14336, 8192], P('section', 'rank'), may hold values from -0.046875 to 0.046875
Outputs:
- next_rows: float32 [2, 16, 8192], P('section', ('groups', 'rank')), parts along dimension 1
There are 2 independent parts, one for each index of `groups`. A program takes and returns all parts, laid end to end along the dimension named above; an argument that names none is the same for every part. Nothing has to cross between parts.
Inputs may be any that keep to these rules, and one draw needn't show every extreme that they name: Each section holds at least one request whose length is 256; lengths vary widely from request to request.
All inputs are finite; a program needn't handle non-finite values.
Results may differ from a plain program's by a relative error of at most 0.0022.
Values may be sent and summed in bfloat16 or wider, within the bound.
A program may use at most 128 MiB of HBM per device.

v0:
```python
import functools

import jax
import jax.numpy as jnp
from jax import lax
from jax.experimental import pallas as pl
from jax.experimental.pallas import tpu as pltpu
from jax.sharding import PartitionSpec as P

HD = 128
EPS = 1e-05
SUB = 32
LANE = 128
SHARE = True
MESH = pl.DeviceIdType.MESH


def attend(q, keys, values, key_new, value_new, length):
    heads, slots = q.shape[0], keys.shape[0]
    kvh = key_new.shape[0]
    per = heads // kvh
    scale = HD ** (-0.5)
    scores, owns = [], []
    for g in range(kvh):
        q_g = q[g * per : (g + 1) * per]
        scores.append(
            lax.dot_general(
                q_g.astype(jnp.bfloat16),
                keys[:, g * HD : (g + 1) * HD],
                (((1,), (1,)), ((), ())),
                preferred_element_type=jnp.float32,
            )
        )
        owns.append(jnp.sum(q_g * key_new[g : g + 1], axis=-1, keepdims=True))
    scores = jnp.concatenate(scores, axis=0) * scale
    own = jnp.concatenate(owns, axis=0) * scale
    live = lax.broadcasted_iota(jnp.int32, (heads, slots), 1) < length
    scores = jnp.where(live, scores, jnp.float32(-1e30))
    top = jnp.maximum(jnp.max(scores, axis=-1, keepdims=True), own)
    powers = jnp.exp(scores - top)
    own_power = jnp.exp(own - top)
    total = jnp.sum(powers, axis=-1, keepdims=True) + own_power
    probs = powers / total
    own_prob = (own_power / total).astype(jnp.bfloat16).astype(jnp.float32)
    out = []
    for g in range(kvh):
        rows = slice(g * per, (g + 1) * per)
        part = jnp.dot(
            probs[rows].astype(jnp.bfloat16),
            values[:, g * HD : (g + 1) * HD],
            preferred_element_type=jnp.float32,
        )
        out.append(part + own_prob[rows] * value_new[g : g + 1])
    return jnp.concatenate(out, axis=0)


def partner(me, step, count):
    if count & (count - 1):
        return lax.rem(me + step, count)
    other, bit = 0, 1
    while bit < count:
        digit = lax.rem(lax.div(me, bit), 2)
        other = other + bit * (1 - digit if step // bit % 2 else digit)
        bit *= 2
    return other


def heads_of(row):
    count = row.shape[1] // HD
    return jnp.concatenate([row[:, h * HD : (h + 1) * HD] for h in range(count)], axis=0)


def layer_kernel(
    sizes, wire,
    len_in, rows_ref, q_ref, kc_ref, vc_ref, kn_ref, vn_ref, gain_ref, up_ref, down_ref,
    out_ref,
    rows_v, q_v, kc_v, vc_v, kn_v, vn_v, gain_v, up_v, down_v,
    mixed_v, mixed_in, gathered, spread, acc, hidden, partial, sending, landed,
    len_ref, small_sem, up_sem, down_sem, mixed_sem, gsend, grecv, rsend, rrecv,
):
    n_groups, n_section, n_rank, share = sizes
    count = n_rank * n_groups if share else n_rank
    group, section, rank = (lax.axis_index(a) for a in ("groups", "section", "rank"))
    me = group * n_rank + rank if share else rank
    chunks = up_v.shape[0]
    width, units = up_v.shape[1], up_v.shape[2]
    first = pl.multiple_of(group * units, LANE) if share else 0
    after = lax.rem(section + 1, n_section)

    def place(peer, which):
        where = {"section": which, "rank": lax.rem(peer, n_rank)}
        if share:
            where["groups"] = lax.div(peer, n_rank)
        return where

    small = [
        pltpu.make_async_copy(src, dst, small_sem.at[i])
        for i, (src, dst) in enumerate(
            (
                (q_ref, q_v), (kc_ref.at[0, 0], kc_v), (kn_ref, kn_v), (vc_ref.at[0, 0], vc_v),
                (vn_ref, vn_v), (rows_ref, rows_v), (gain_ref, gain_v), (len_in, len_ref),
            )
        )
    ]
    for copy in small:
        copy.start()
    ups = [
        pltpu.make_async_copy(
            up_ref.at[0, pl.ds(c * width, width), pl.ds(first, units)], up_v.at[c], up_sem.at[c]
        )
        for c in range(chunks)
    ]
    downs = [
        pltpu.make_async_copy(
            down_ref.at[0, pl.ds(first, units), pl.ds(c * width, width)],
            down_v.at[c],
            down_sem.at[c],
        )
        for c in range(chunks)
    ]
    for copy in ups + downs:
        copy.start()

    barrier = pltpu.get_barrier_semaphore()
    for shift in range(n_section):
        for step in range(count):
            if shift or step:
                pl.semaphore_signal(
                    barrier,
                    inc=1,
                    device_id=place(partner(me, step, count), lax.rem(section + shift, n_section)),
                    device_id_type=MESH,
                )

    for copy in small:
        copy.wait()
    attended = attend(
        heads_of(q_v[0].astype(jnp.float32)),
        kc_v[...],
        vc_v[...],
        heads_of(kn_v[0].astype(jnp.float32)),
        heads_of(vn_v[0].astype(jnp.float32)),
        len_ref[0, 0],
    )
    mixed = rows_v[...] + attended
    mixed_v[...] = mixed
    square = jnp.sum(jnp.sum(mixed * mixed, axis=-1, keepdims=True), axis=0, keepdims=True)
    scaled = mixed * lax.rsqrt(square / (mixed.shape[0] * mixed.shape[1]) + EPS)
    normed = (scaled * gain_v[...]).astype(jnp.bfloat16)
    for c in range(chunks):
        gathered[me, c] = normed[c * SUB : (c + 1) * SUB]

    pl.semaphore_wait(barrier, n_section * count - 1)

    def row_copy(c, peer, owner):
        return pltpu.make_async_remote_copy(
            src_ref=gathered.at[owner, c],
            dst_ref=gathered.at[owner, c],
            send_sem=gsend.at[peer, c],
            recv_sem=grecv.at[owner, c],
            device_id=place(peer, section),
            device_id_type=MESH,
        )

    @pl.loop(0, chunks)
    def _(c):
        for step in range(count - 1, 0, -1):
            row_copy(c, partner(me, step, count), me).start()

    mixed_copy = pltpu.make_async_remote_copy(
        src_ref=mixed_v,
        dst_ref=mixed_in,
        send_sem=mixed_sem.at[0],
        recv_sem=mixed_sem.at[1],
        device_id=place(me, after),
        device_id_type=MESH,
    )
    mixed_copy.start()

    acc[...] = jnp.zeros_like(acc)

    @pl.loop(0, chunks)
    def _(c):
        for step in range(1, count):
            row_copy(c, me, partner(me, step, count)).wait_recv()
        for r in range(count):
            spread[r * SUB : (r + 1) * SUB] = gathered[r, c].astype(jnp.float32)
        block = jnp.concatenate(
            [spread[pl.ds(j, count, stride=SUB), :] for j in range(SUB)], axis=1
        ).astype(jnp.bfloat16)
        pltpu.make_async_copy(
            up_ref.at[0, pl.ds(0, width), pl.ds(first, units)], up_v.at[c], up_sem.at[c]
        ).wait()
        acc[...] += jnp.dot(block, up_v[c], preferred_element_type=jnp.float32)

    upward = acc[...]
    hidden[...] = (upward / (1.0 + jnp.exp(-upward))).astype(jnp.bfloat16)

    def part_copy(c, peer, owner):
        return pltpu.make_async_remote_copy(
            src_ref=sending.at[c, pl.ds(pl.multiple_of(peer * SUB, SUB), SUB)],
            dst_ref=landed.at[owner, c],
            send_sem=rsend.at[peer, c],
            recv_sem=rrecv.at[owner, c],
            device_id=place(peer, after),
            device_id_type=MESH,
        )

    @pl.loop(0, chunks)
    def _(c):
        pltpu.make_async_copy(
            down_ref.at[0, pl.ds(first, units), pl.ds(0, width)], down_v.at[c], down_sem.at[c]
        ).wait()
        lowered = jnp.dot(hidden[...], down_v[c], preferred_element_type=jnp.float32)
        for j in range(SUB):
            partial[pl.ds(j, count, stride=SUB), :] = lowered[:, j * LANE : (j + 1) * LANE]
        sending[c] = partial[...].astype(wire)
        for step in range(count - 1, -1, -1):
            part_copy(c, partner(me, step, count), me).start()

    mixed_copy.wait_recv()

    @pl.loop(0, chunks)
    def _(c):
        total = mixed_in[pl.ds(pl.multiple_of(c * SUB, SUB), SUB)]
        for step in range(count):
            part_copy(c, me, partner(me, step, count)).wait_recv()
        for r in range(count):
            total = total + landed[r, c].astype(jnp.float32)
        out_ref[pl.ds(pl.multiple_of(c * SUB, SUB), SUB)] = total

    mixed_copy.wait_send()

    @pl.loop(0, chunks)
    def _(c):
        for step in range(count):
            peer = partner(me, step, count)
            if step:
                row_copy(c, peer, me).wait_send()
            part_copy(c, peer, me).wait_send()


def fused(
    mesh_sizes, rows_in, query, key_cache, value_cache, key_new, value_new, lengths, norm_gain,
    w_up, w_down,
):
    n_groups, n_section, n_rank, share = mesh_sizes
    count = n_rank * n_groups if share else n_rank
    wire = jnp.bfloat16 if share else jnp.float32
    d, slots, kv = rows_in.shape[-1], key_cache.shape[2], key_cache.shape[3]
    units = w_up.shape[2] // (n_groups if share else 1)
    heads, kvh = d // HD, kv // HD
    width = SUB * LANE
    chunks = d // width
    f32, bf16 = jnp.float32, jnp.bfloat16
    anywhere = pl.BlockSpec(memory_space=pl.ANY)
    out = pl.pallas_call(
        functools.partial(layer_kernel, mesh_sizes, wire),
        out_shape=jax.ShapeDtypeStruct((heads, HD), f32),
        in_specs=[anywhere] * 10,
        out_specs=pl.BlockSpec(memory_space=pltpu.VMEM),
        scratch_shapes=[
            pltpu.VMEM((heads, HD), f32),
            pltpu.VMEM((1, 1, d), bf16),
            pltpu.VMEM((slots, kv), bf16),
            pltpu.VMEM((slots, kv), bf16),
            pltpu.VMEM((1, 1, kv), bf16),
            pltpu.VMEM((1, 1, kv), bf16),
            pltpu.VMEM((heads, HD), f32),
            pltpu.VMEM((chunks, width, units), bf16),
            pltpu.VMEM((chunks, units, width), bf16),
            pltpu.VMEM((heads, HD), f32),
            pltpu.VMEM((heads, HD), f32),
            pltpu.VMEM((count, chunks, SUB, LANE), bf16),
            pltpu.VMEM((count * SUB, LANE), f32),
            pltpu.VMEM((count, units), f32),
            pltpu.VMEM((count, units), bf16),
            pltpu.VMEM((count * SUB, LANE), f32),
            pltpu.VMEM((chunks, count * SUB, LANE), wire),
            pltpu.VMEM((count, chunks, SUB, LANE), wire),
            pltpu.SMEM((1, 1), jnp.int32),
            pltpu.SemaphoreType.DMA((8,)),
            pltpu.SemaphoreType.DMA((chunks,)),
            pltpu.SemaphoreType.DMA((chunks,)),
            pltpu.SemaphoreType.DMA((2,)),
            pltpu.SemaphoreType.DMA((count, chunks)),
            pltpu.SemaphoreType.DMA((count, chunks)),
            pltpu.SemaphoreType.DMA((count, chunks)),
            pltpu.SemaphoreType.DMA((count, chunks)),
        ],
        compiler_params=pltpu.CompilerParams(
            collective_id=0, has_side_effects=True, vmem_limit_bytes=64 * 1024 * 1024 - 65536
        ),
        name="layer",
    )(
        lengths,
        rows_in.reshape(heads, HD),
        query,
        key_cache,
        value_cache,
        key_new,
        value_new,
        norm_gain.reshape(heads, HD),
        w_up,
        w_down,
    )
    return out.reshape(1, 1, d)


def attend_plain(query, key_cache, value_cache, key_new, value_new, length):
    kv = key_cache.shape[1] // HD
    out = attend(
        query.reshape(-1, HD).astype(jnp.float32),
        key_cache,
        value_cache,
        key_new.reshape(kv, HD).astype(jnp.float32),
        value_new.reshape(kv, HD).astype(jnp.float32),
        length,
    )
    return out.reshape(-1)


def plain(
    rows_in, query, key_cache, value_cache, key_new, value_new, lengths, norm_gain, w_up, w_down
):
    section_rows = rows_in[0]
    local_rows = section_rows.shape[0]
    attended = jax.vmap(attend_plain)(
        query[0], key_cache[0], value_cache[0], key_new[0], value_new[0], lengths[0]
    )
    mixed = section_rows + attended
    scaled = mixed * lax.rsqrt(jnp.mean(mixed * mixed, axis=-1, keepdims=True) + EPS)
    normed = (scaled * norm_gain[0][None, :]).astype(jnp.bfloat16)
    upward = jnp.dot(
        lax.all_gather(normed, "rank", axis=0, tiled=True),
        w_up[0],
        preferred_element_type=jnp.float32,
    )
    hidden = jax.nn.silu(upward).astype(jnp.bfloat16)
    whole = lax.psum(jnp.dot(hidden, w_down[0], preferred_element_type=jnp.float32), "rank")
    mine = lax.dynamic_slice_in_dim(whole, lax.axis_index("rank") * local_rows, local_rows, 0)
    size = lax.axis_size("section")
    pairs = [(source, (source + 1) % size) for source in range(size)]
    return lax.ppermute(mixed + mine, "section", pairs)[None]


def solution(mesh):
    n_groups, n_section, n_rank = (mesh.shape[a] for a in ("groups", "section", "rank"))
    sizes = (n_groups, n_section, n_rank, SHARE)

    def per_device(*args):
        rows, d = args[0].shape[1], args[0].shape[2]
        units = args[8].shape[2] // (n_groups if SHARE else 1)
        fits = (
            rows == 1
            and n_section > 1
            and units % LANE == 0
            and d % (SUB * LANE) == 0
            and n_rank * n_groups <= 32
            and 4 * d * units < 60 * 1000 * 1000
        )
        if fits:
            return fused(sizes, *args)
        return plain(*args)

    placed = (
        P("section", ("groups", "rank"), None),
        P("section", ("groups", "rank"), None),
        P("section", ("groups", "rank"), None, None),
        P("section", ("groups", "rank"), None, None),
        P("section", ("groups", "rank"), None),
        P("section", ("groups", "rank"), None),
        P("section", ("groups", "rank")),
        P("section", None),
        P("section", None, "rank"),
        P("section", "rank", None),
    )
    return jax.shard_map(
        per_device,
        mesh=mesh,
        in_specs=placed,
        out_specs=P("section", ("groups", "rank"), None),
        check_vma=False,
    )
```

profile of v0, /device:TPU:1, one launch (start us, length us, event | category | flops | bytes accessed | tf_op | source)
XLA Modules:
  0.0 28.4 jit_solution(15410443388782294195)
XLA Ops:
  0.7 26.4 %layer.1 = f32[64,128]{1,0:T(8,128)} custom-call(s32[1,1]{1,0:T(1,128)S(6)} %copy.12.len_in, f32[64,128]{1,0:T(8,128)} %bitcast.4, bf16[1,1,8192]{2,1,0:T(2,128)(2,1)} %q_ref.1, bf16[1,1,256,1024]{3,2,1,0:T(8,128)(2,1)} %kc_ref.1, bf16[1,1,256,1024]{3,2,1,0:T(8,128)(2,1)} %vc_ref.1, bf16[1,1,1024]{2,1,0:T(2,128)(2,1)} %kn_ref.1, bf16[1,1,1024]{2,1,0:T(2,128)(2,1)} %vn_ref.1, ...), custom_call_target="tpu_custom_call" | custom-call | tf_op jit(solution)/shard_map/layer/pallas_call | solution.py:257
  27.0 1.4 %copy.13 = f32[1,1,8192]{2,1,0:T(1,128)} copy(f32[1,1,8192]{2,1,0:T(1,128)} %bitcast.3) | data formatting | bytes 65536
where the time goes:
time: 28.6 us; the launch traced here: 28.4 us
  Pallas kernels  26.4 us (92%)
  local copies, waits for them, and re-layouts  1.38 us (5%)
  between operations  0.66 us (2%)
    pallas_call x1, Pallas kernels, fused(): pl.pallas_call(functools.partial(layer_kernel, mesh_sizes, wire), out_sha...  26.4 us
    unnamed x1, local copies, waits for them, and re-layouts  1.38 us

commit v1 on v0

v1 whole, which is shorter than its diff:
```python
import functools

import jax
import jax.numpy as jnp
from jax import lax
from jax.experimental import pallas as pl
from jax.experimental.pallas import tpu as pltpu
from jax.sharding import PartitionSpec as P

HD = 128
EPS = 1e-05
LANE = 128
KV_CUTS = 2
ROW_CHUNKS = 2
UP_CHUNKS = 4
DOWN_CHUNKS = 4
PIECES = 2
MESH = pl.DeviceIdType.MESH


def attend(q, keys, values, key_new, value_new, length):
    heads, slots = q.shape[0], keys.shape[0]
    kvh = key_new.shape[0]
    per = heads // kvh
    scale = HD ** (-0.5)
    scores, owns = [], []
    for g in range(kvh):
        q_g = q[g * per : (g + 1) * per]
        scores.append(
            lax.dot_general(
                q_g.astype(jnp.bfloat16),
                keys[:, g * HD : (g + 1) * HD],
                (((1,), (1,)), ((), ())),
                preferred_element_type=jnp.float32,
            )
        )
        owns.append(jnp.sum(q_g * key_new[g : g + 1], axis=-1, keepdims=True))
    scores = jnp.concatenate(scores, axis=0) * scale
    own = jnp.concatenate(owns, axis=0) * scale
    live = lax.broadcasted_iota(jnp.int32, (heads, slots), 1) < length
    scores = jnp.where(live, scores, jnp.float32(-1e30))
    top = jnp.maximum(jnp.max(scores, axis=-1, keepdims=True), own)
    powers = jnp.exp(scores - top)
    own_power = jnp.exp(own - top)
    total = jnp.sum(powers, axis=-1, keepdims=True) + own_power
    probs = powers / total
    own_prob = (own_power / total).astype(jnp.bfloat16).astype(jnp.float32)
    out = []
    for g in range(kvh):
        rows = slice(g * per, (g + 1) * per)
        part = jnp.dot(
            probs[rows].astype(jnp.bfloat16),
            values[:, g * HD : (g + 1) * HD],
            preferred_element_type=jnp.float32,
        )
        out.append(part + own_prob[rows] * value_new[g : g + 1])
    return jnp.concatenate(out, axis=0)


def partner(me, step, count):
    other, bit = 0, 1
    while bit < count:
        digit = lax.rem(lax.div(me, bit), 2)
        other = other + bit * (1 - digit if step // bit % 2 else digit)
        bit *= 2
    return other


def far_first(n_groups, n_rank):
    steps = range(n_groups * n_rank)
    return sorted(steps, key=lambda s: (-(s % n_rank // 2), -(s // n_rank), -(s % 2)))


def heads_of(row):
    count = row.shape[1] // HD
    return jnp.concatenate([row[:, h * HD : (h + 1) * HD] for h in range(count)], axis=0)


def layer_kernel(
    sizes, pieces,
    len_in, rows_ref, q_ref, kc_ref, vc_ref, kn_ref, vn_ref, gain_ref, up_ref, down_ref,
    out_ref,
    rows_v, q_v, kc_v, vc_v, kn_v, vn_v, gain_v, up_v, down_v,
    mixed_v, mixed_in, mine, gathered, spread, acc, passing, passed, hidden, partial, sending,
    landed,
    len_ref, small_sem, kv_sem, up_sem, down_sem, mixed_sem, gsend, grecv, xsem, rsend, rrecv,
):
    n_groups, n_section, n_rank = sizes
    count = n_rank * n_groups
    group, section, rank = (lax.axis_index(a) for a in ("groups", "section", "rank"))
    me = group * n_rank + rank
    after = lax.rem(section + 1, n_section)
    order = far_first(n_groups, n_rank)
    up_chunks, depth = up_v.shape[0], up_v.shape[1]
    down_chunks, width = down_v.shape[0], down_v.shape[2]
    row_chunks, row_sub = gathered.shape[0], gathered.shape[2]
    part_sub = width // LANE
    half = up_chunks * depth
    base = pl.multiple_of(group * half, LANE)

    def place(peer, which):
        return {
            "groups": lax.div(peer, n_rank), "section": which, "rank": lax.rem(peer, n_rank)
        }

    small = [
        pltpu.make_async_copy(src, dst, small_sem.at[i])
        for i, (src, dst) in enumerate(
            (
                (q_ref, q_v), (kn_ref, kn_v), (len_in, len_ref),
                (vn_ref, vn_v), (rows_ref, rows_v), (gain_ref, gain_v),
            )
        )
    ]
    cut = kc_v.shape[0] // KV_CUTS
    caches = [
        pltpu.make_async_copy(
            ref.at[0, 0, pl.ds(i * cut, cut)], dst.at[pl.ds(i * cut, cut)], kv_sem.at[which, i]
        )
        for which, (ref, dst) in enumerate(((kc_ref, kc_v), (vc_ref, vc_v)))
        for i in range(KV_CUTS)
    ]
    for copy in small[:3] + caches[:KV_CUTS] + small[3:] + caches[KV_CUTS:]:
        copy.start()

    barrier = pltpu.get_barrier_semaphore()
    for shift in range(n_section):
        for step in range(count):
            if shift or step:
                pl.semaphore_signal(
                    barrier,
                    inc=1,
                    device_id=place(partner(me, step, count), lax.rem(section + shift, n_section)),
                    device_id_type=MESH,
                )

    ups = [
        pltpu.make_async_copy(
            up_ref.at[0, pl.ds(base + c * depth, depth)], up_v.at[c], up_sem.at[c]
        )
        for c in range(up_chunks)
    ]
    downs = [
        pltpu.make_async_copy(
            down_ref.at[0, :, pl.ds(base + c * width, width)], down_v.at[c], down_sem.at[c]
        )
        for c in range(down_chunks)
    ]
    for copy in ups + downs:
        copy.start()

    for copy in small + caches:
        copy.wait()
    attended = attend(
        heads_of(q_v[0].astype(jnp.float32)),
        kc_v[...],
        vc_v[...],
        heads_of(kn_v[0].astype(jnp.float32)),
        heads_of(vn_v[0].astype(jnp.float32)),
        len_ref[0, 0],
    )
    mixed = rows_v[...] + attended
    mixed_v[...] = mixed
    square = jnp.sum(jnp.sum(mixed * mixed, axis=-1, keepdims=True), axis=0, keepdims=True)
    scaled = mixed * lax.rsqrt(square / (mixed.shape[0] * mixed.shape[1]) + EPS)
    normed = (scaled * gain_v[...]).astype(jnp.bfloat16)
    for p in range(n_groups):
        for c in range(row_chunks):
            at = (p * row_chunks + c) * row_sub
            mine[p, c] = normed[at : at + row_sub]

    pl.semaphore_wait(barrier, n_section * count - 1)

    def row_copy(c, peer):
        return pltpu.make_async_remote_copy(
            src_ref=mine.at[lax.div(peer, n_rank), c],
            dst_ref=gathered.at[c, me],
            send_sem=gsend.at[c, peer],
            recv_sem=grecv.at[c, me],
            device_id=place(peer, section),
            device_id_type=MESH,
        )

    def row_landing(c, owner):
        return pltpu.make_async_remote_copy(
            src_ref=mine.at[0, c],
            dst_ref=gathered.at[c, owner],
            send_sem=gsend.at[c, owner],
            recv_sem=grecv.at[c, owner],
            device_id=place(owner, section),
            device_id_type=MESH,
        )

    @pl.loop(0, row_chunks)
    def _(c):
        for step in order:
            if step:
                row_copy(c, partner(me, step, count)).start()

    mixed_copy = pltpu.make_async_remote_copy(
        src_ref=mixed_v,
        dst_ref=mixed_in,
        send_sem=mixed_sem.at[0],
        recv_sem=mixed_sem.at[1],
        device_id=place(me, after),
        device_id_type=MESH,
    )
    mixed_copy.start()
    for c in range(row_chunks):
        gathered[c, me] = mine[group, c]

    def rows_of(c):
        for step in range(1, count):
            row_landing(c, partner(me, step, count)).wait_recv()
        for r in range(count):
            spread[r * row_sub : (r + 1) * row_sub] = gathered[c, r].astype(jnp.float32)
        return jnp.concatenate(
            [spread[pl.ds(j, count, stride=row_sub), :] for j in range(row_sub)], axis=1
        ).astype(jnp.bfloat16)

    def piece_copy(p):
        at, size = pieces[p]
        return pltpu.make_async_remote_copy(
            src_ref=passing.at[:, pl.ds(at, size)],
            dst_ref=passed.at[:, pl.ds(at, size)],
            send_sem=xsem.at[0, p],
            recv_sem=xsem.at[1, p],
            device_id={"groups": 1 - group, "section": section, "rank": rank},
            device_id_type=MESH,
        )

    per = up_chunks // row_chunks
    for c in range(row_chunks):
        block = rows_of(c)
        for k in range(per):
            ups[c * per + k].wait()
        weights = [up_v.at[c * per + k] for k in range(per)]
        blocks = [block[:, k * depth : (k + 1) * depth] for k in range(per)]
        last = c == row_chunks - 1
        for p, (at, size) in enumerate(pieces):
            total = acc[:, at : at + size] if c else 0.0
            for k in range(per):
                total = total + jnp.dot(
                    blocks[k], weights[k][:, at : at + size], preferred_element_type=jnp.float32
                )
            acc[:, at : at + size] = total
            if last:
                passing[:, at : at + size] = total.astype(jnp.bfloat16)
                piece_copy(p).start()

    for p, (at, size) in enumerate(pieces):
        piece_copy(p).wait_recv()
        upward = acc[:, at : at + size] + passed[:, at : at + size].astype(jnp.float32)
        hidden[:, at : at + size] = (upward / (1.0 + jnp.exp(-upward))).astype(jnp.bfloat16)

    def part_copy(c, peer):
        return pltpu.make_async_remote_copy(
            src_ref=sending.at[c, peer],
            dst_ref=landed.at[me, c],
            send_sem=rsend.at[c, peer],
            recv_sem=rrecv.at[c, me],
            device_id=place(peer, after),
            device_id_type=MESH,
        )

    def part_landing(c, owner):
        return pltpu.make_async_remote_copy(
            src_ref=sending.at[c, owner],
            dst_ref=landed.at[owner, c],
            send_sem=rsend.at[c, owner],
            recv_sem=rrecv.at[c, owner],
            device_id=place(owner, after),
            device_id_type=MESH,
        )

    @pl.loop(0, down_chunks)
    def _(c):
        pltpu.make_async_copy(
            down_ref.at[0, :, pl.ds(0, width)], down_v.at[c], down_sem.at[c]
        ).wait()
        lowered = jnp.dot(hidden[...], down_v[c], preferred_element_type=jnp.float32)
        for j in range(part_sub):
            partial[pl.ds(j, count, stride=part_sub), :] = lowered[:, j * LANE : (j + 1) * LANE]
        for r in range(count):
            sending[c, r] = partial[r * part_sub : (r + 1) * part_sub].astype(jnp.bfloat16)
        for step in order:
            part_copy(c, partner(me, step, count)).start()

    mixed_copy.wait_recv()

    @pl.loop(0, down_chunks)
    def _(c):
        for step in range(count):
            part_landing(c, partner(me, step, count)).wait_recv()
        for p in range(n_groups):
            rows = pl.ds(pl.multiple_of((p * down_chunks + c) * part_sub, part_sub), part_sub)
            total = mixed_in[rows]
            for r in range(n_rank):
                total = total + landed[p * n_rank + r, c].astype(jnp.float32)
            out_ref[rows] = total

    mixed_copy.wait_send()
    for p in range(len(pieces)):
        piece_copy(p).wait_send()

    @pl.loop(0, row_chunks)
    def _(c):
        for step in range(1, count):
            row_landing(c, partner(me, step, count)).wait_send()

    @pl.loop(0, down_chunks)
    def _(c):
        for step in range(count):
            part_landing(c, partner(me, step, count)).wait_send()


def fused(
    mesh_sizes, rows_in, query, key_cache, value_cache, key_new, value_new, lengths, norm_gain,
    w_up, w_down,
):
    n_groups, n_section, n_rank = mesh_sizes
    count = n_rank * n_groups
    d, slots, kv = rows_in.shape[-1], key_cache.shape[2], key_cache.shape[3]
    units = w_up.shape[2]
    heads, kvh, half = d // HD, kv // HD, d // n_groups
    depth, width = half // UP_CHUNKS, half // DOWN_CHUNKS
    row_sub, part_sub = half // ROW_CHUNKS // LANE, width // LANE
    first = -(-units // (256 * PIECES)) * 256
    pieces = [(at, min(first, units - at)) for at in range(0, units, first)]
    f32, bf16 = jnp.float32, jnp.bfloat16
    anywhere = pl.BlockSpec(memory_space=pltpu.HBM)
    out = pl.pallas_call(
        functools.partial(layer_kernel, mesh_sizes, pieces),
        out_shape=jax.ShapeDtypeStruct((heads, HD), f32),
        in_specs=[anywhere] * 10,
        out_specs=pl.BlockSpec(memory_space=pltpu.VMEM),
        scratch_shapes=[
            pltpu.VMEM((heads, HD), f32),
            pltpu.VMEM((1, 1, d), bf16),
            pltpu.VMEM((slots, kv), bf16),
            pltpu.VMEM((slots, kv), bf16),
            pltpu.VMEM((1, 1, kv), bf16),
            pltpu.VMEM((1, 1, kv), bf16),
            pltpu.VMEM((heads, HD), f32),
            pltpu.VMEM((UP_CHUNKS, depth, units), bf16),
            pltpu.VMEM((DOWN_CHUNKS, units, width), bf16),
            pltpu.VMEM((heads, HD), f32),
            pltpu.VMEM((heads, HD), f32),
            pltpu.VMEM((n_groups, ROW_CHUNKS, row_sub, LANE), bf16),
            pltpu.VMEM((ROW_CHUNKS, count, row_sub, LANE), bf16),
            pltpu.VMEM((count * row_sub, LANE), f32),
            pltpu.VMEM((count, units), f32),
            pltpu.VMEM((count, units), bf16),
            pltpu.VMEM((count, units), bf16),
            pltpu.VMEM((count, units), bf16),
            pltpu.VMEM((count * part_sub, LANE), f32),
            pltpu.VMEM((DOWN_CHUNKS, count, part_sub, LANE), bf16),
            pltpu.VMEM((count, DOWN_CHUNKS, part_sub, LANE), bf16),
            pltpu.SMEM((1, 1), jnp.int32),
            pltpu.SemaphoreType.DMA((6,)),
            pltpu.SemaphoreType.DMA((2, KV_CUTS)),
            pltpu.SemaphoreType.DMA((UP_CHUNKS,)),
            pltpu.SemaphoreType.DMA((DOWN_CHUNKS,)),
            pltpu.SemaphoreType.DMA((2,)),
            pltpu.SemaphoreType.DMA((ROW_CHUNKS, count)),
            pltpu.SemaphoreType.DMA((ROW_CHUNKS, count)),
            pltpu.SemaphoreType.DMA((2, len(pieces))),
            pltpu.SemaphoreType.DMA((DOWN_CHUNKS, count)),
            pltpu.SemaphoreType.DMA((DOWN_CHUNKS, count)),
        ],
        compiler_params=pltpu.CompilerParams(
            collective_id=0, has_side_effects=True, vmem_limit_bytes=64 * 1024 * 1024 - 65536
        ),
        name="layer",
    )(
        lengths,
        rows_in.reshape(heads, HD),
        query,
        key_cache,
        value_cache,
        key_new,
        value_new,
        norm_gain.reshape(heads, HD),
        w_up,
        w_down,
    )
    return out.reshape(1, 1, d)


def attend_plain(query, key_cache, value_cache, key_new, value_new, length):
    kv = key_cache.shape[1] // HD
    out = attend(
        query.reshape(-1, HD).astype(jnp.float32),
        key_cache,
        value_cache,
        key_new.reshape(kv, HD).astype(jnp.float32),
        value_new.reshape(kv, HD).astype(jnp.float32),
        length,
    )
    return out.reshape(-1)


def plain(
    rows_in, query, key_cache, value_cache, key_new, value_new, lengths, norm_gain, w_up, w_down
):
    section_rows = rows_in[0]
    local_rows = section_rows.shape[0]
    attended = jax.vmap(attend_plain)(
        query[0], key_cache[0], value_cache[0], key_new[0], value_new[0], lengths[0]
    )
    mixed = section_rows + attended
    scaled = mixed * lax.rsqrt(jnp.mean(mixed * mixed, axis=-1, keepdims=True) + EPS)
    normed = (scaled * norm_gain[0][None, :]).astype(jnp.bfloat16)
    upward = jnp.dot(
        lax.all_gather(normed, "rank", axis=0, tiled=True),
        w_up[0],
        preferred_element_type=jnp.float32,
    )
    hidden = jax.nn.silu(upward).astype(jnp.bfloat16)
    whole = lax.psum(jnp.dot(hidden, w_down[0], preferred_element_type=jnp.float32), "rank")
    mine = lax.dynamic_slice_in_dim(whole, lax.axis_index("rank") * local_rows, local_rows, 0)
    size = lax.axis_size("section")
    pairs = [(source, (source + 1) % size) for source in range(size)]
    return lax.ppermute(mixed + mine, "section", pairs)[None]


def solution(mesh):
    n_groups, n_section, n_rank = (mesh.shape[a] for a in ("groups", "section", "rank"))
    sizes = (n_groups, n_section, n_rank)
    count = n_groups * n_rank

    def per_device(*args):
        rows, d = args[0].shape[1], args[0].shape[2]
        slots, units = args[2].shape[2], args[8].shape[2]
        fits = (
            rows == 1
            and n_groups == 2
            and n_section > 1
            and count & (count - 1) == 0
            and count <= 32
            and units % LANE == 0
            and slots % (16 * KV_CUTS) == 0
            and d % (16 * LANE * n_groups * ROW_CHUNKS) == 0
            and d % (LANE * n_groups * UP_CHUNKS) == 0
            and d % (8 * LANE * n_groups * DOWN_CHUNKS) == 0
            and 4 * d // n_groups * units < 60 * 1000 * 1000
        )
        if fits:
            return fused(sizes, *args)
        return plain(*args)

    placed = (
        P("section", ("groups", "rank"), None),
        P("section", ("groups", "rank"), None),
        P("section", ("groups", "rank"), None, None),
        P("section", ("groups", "rank"), None, None),
        P("section", ("groups", "rank"), None),
        P("section", ("groups", "rank"), None),
        P("section", ("groups", "rank")),
        P("section", None),
        P("section", None, "rank"),
        P("section", "rank", None),
    )
    return jax.shard_map(
        per_device,
        mesh=mesh,
        in_specs=placed,
        out_specs=P("section", ("groups", "rank"), None),
        check_vma=False,
    )
```

time: 28.6 us -> 28.5 us (level)
  no operation moved by 1% of the time
where the time goes in v1:
time: 28.5 us; the launch traced here: 28.3 us
  Pallas kernels  26.2 us (92%)
  local copies, waits for them, and re-layouts  1.38 us (5%)
  between operations  0.66 us (2%)
    pallas_call x1, Pallas kernels, fused(): pl.pallas_call(functools.partial(layer_kernel, mesh_sizes, pieces), out_s...  26.2 us
    unnamed x1, local copies, waits for them, and re-layouts  1.38 us

profile of v1, /device:TPU:1, one launch (start us, length us, event | category | flops | bytes accessed | tf_op | source)
XLA Modules:
  0.0 28.3 jit_solution(3203071446297889466)
XLA Ops:
  0.7 26.2 %layer.1 = f32[64,128]{1,0:T(8,128)} custom-call(s32[1,1]{1,0:T(1,128)S(6)} %copy.12.len_in, f32[64,128]{1,0:T(8,128)} %bitcast.4, bf16[1,1,8192]{2,1,0:T(2,128)(2,1)} %q_ref.1, bf16[1,1,256,1024]{3,2,1,0:T(8,128)(2,1)} %kc_ref.1, bf16[1,1,256,1024]{3,2,1,0:T(8,128)(2,1)} %vc_ref.1, bf16[1,1,1024]{2,1,0:T(2,128)(2,1)} %kn_ref.1, bf16[1,1,1024]{2,1,0:T(2,128)(2,1)} %vn_ref.1, ...), custom_call_target="tpu_custom_call" | custom-call | tf_op jit(solution)/shard_map/layer/pallas_call | solution.py:332
  26.9 1.4 %copy.13 = f32[1,1,8192]{2,1,0:T(1,128)} copy(f32[1,1,8192]{2,1,0:T(1,128)} %bitcast.3) | data formatting | bytes 65536

commit v2 on v1

v2 whole, which is shorter than its diff:
```python
import functools

import jax
import jax.numpy as jnp
from jax import lax
from jax.experimental import pallas as pl
from jax.experimental.pallas import tpu as pltpu
from jax.sharding import PartitionSpec as P

HD = 128
EPS = 1e-05
LANE = 128
UP_CHUNKS = 4
PIECE = 512
WIDTH = 1024
MESH = pl.DeviceIdType.MESH


def attend(q, keys, values, key_new, value_new, length):
    heads, slots = q.shape[0], keys.shape[0]
    kvh = key_new.shape[0]
    per = heads // kvh
    scale = HD ** (-0.5)
    scores, owns = [], []
    for g in range(kvh):
        q_g = q[g * per : (g + 1) * per]
        scores.append(
            lax.dot_general(
                q_g.astype(jnp.bfloat16),
                keys[:, g * HD : (g + 1) * HD],
                (((1,), (1,)), ((), ())),
                preferred_element_type=jnp.float32,
            )
        )
        owns.append(jnp.sum(q_g * key_new[g : g + 1], axis=-1, keepdims=True))
    scores = jnp.concatenate(scores, axis=0) * scale
    own = jnp.concatenate(owns, axis=0) * scale
    live = lax.broadcasted_iota(jnp.int32, (heads, slots), 1) < length
    scores = jnp.where(live, scores, jnp.float32(-1e30))
    top = jnp.maximum(jnp.max(scores, axis=-1, keepdims=True), own)
    powers = jnp.exp(scores - top)
    own_power = jnp.exp(own - top)
    total = jnp.sum(powers, axis=-1, keepdims=True) + own_power
    probs = powers / total
    own_prob = (own_power / total).astype(jnp.bfloat16).astype(jnp.float32)
    out = []
    for g in range(kvh):
        rows = slice(g * per, (g + 1) * per)
        part = jnp.dot(
            probs[rows].astype(jnp.bfloat16),
            values[:, g * HD : (g + 1) * HD],
            preferred_element_type=jnp.float32,
        )
        out.append(part + own_prob[rows] * value_new[g : g + 1])
    return jnp.concatenate(out, axis=0)


def partner(me, step, count):
    other, bit = 0, 1
    while bit < count:
        digit = lax.rem(lax.div(me, bit), 2)
        other = other + bit * (1 - digit if step // bit % 2 else digit)
        bit *= 2
    return other


def far_first(n_groups, n_rank):
    steps = range(n_groups * n_rank)
    return sorted(steps, key=lambda s: (-(s % n_rank // 2), -(s // n_rank), -(s % 2)))


def heads_of(row):
    count = row.shape[1] // HD
    return jnp.concatenate([row[:, h * HD : (h + 1) * HD] for h in range(count)], axis=0)


def layer_kernel(
    sizes, pieces,
    len_in, rows_ref, q_ref, kc_ref, vc_ref, kn_ref, vn_ref, gain_ref, up_ref, down_ref,
    out_ref,
    rows_v, q_v, kc_v, vc_v, kn_v, vn_v, gain_v, up_v, down_v,
    mixed_v, mixed_in, mine, gathered, spread, acc, passing, passed, lowered, sending, landed,
    len_ref, small_sem, up_sem, down_sem, mixed_sem, gather_sem, piece_sem, part_sem,
):
    n_groups, n_section, n_rank = sizes
    count = n_rank * n_groups
    group, section, rank = (lax.axis_index(a) for a in ("groups", "section", "rank"))
    me = group * n_rank + rank
    after = lax.rem(section + 1, n_section)
    order = far_first(n_groups, n_rank)
    up_chunks, depth = up_v.shape[0], up_v.shape[1]
    half = up_chunks * depth
    sub = half // LANE
    base = pl.multiple_of(group * half, LANE)

    def place(peer, which):
        return {
            "groups": lax.div(peer, n_rank), "section": which, "rank": lax.rem(peer, n_rank)
        }

    small = [
        pltpu.make_async_copy(src, dst, small_sem.at[i])
        for i, (src, dst) in enumerate(
            (
                (q_ref, q_v), (kc_ref.at[0, 0], kc_v), (kn_ref, kn_v), (len_in, len_ref),
                (vc_ref.at[0, 0], vc_v), (vn_ref, vn_v), (rows_ref, rows_v), (gain_ref, gain_v),
            )
        )
    ]
    for copy in small:
        copy.start()

    barrier = pltpu.get_barrier_semaphore()
    for step in order:
        for shift in range(n_section):
            if shift or step:
                pl.semaphore_signal(
                    barrier,
                    inc=1,
                    device_id=place(partner(me, step, count), lax.rem(section + shift, n_section)),
                    device_id_type=MESH,
                )

    ups = [
        pltpu.make_async_copy(
            up_ref.at[0, pl.ds(base + c * depth, depth)], up_v.at[c], up_sem.at[c]
        )
        for c in range(up_chunks)
    ]
    downs = [
        pltpu.make_async_copy(
            down_ref.at[0, pl.ds(at, size), pl.ds(base, half)],
            down_v.at[pl.ds(at, size)],
            down_sem.at[p],
        )
        for p, (at, size) in enumerate(pieces)
    ]
    for copy in ups + downs:
        copy.start()

    for copy in small:
        copy.wait()
    attended = attend(
        heads_of(q_v[0].astype(jnp.float32)),
        kc_v[...],
        vc_v[...],
        heads_of(kn_v[0].astype(jnp.float32)),
        heads_of(vn_v[0].astype(jnp.float32)),
        len_ref[0, 0],
    )
    mixed = rows_v[...] + attended
    mixed_v[...] = mixed
    square = jnp.sum(jnp.sum(mixed * mixed, axis=-1, keepdims=True), axis=0, keepdims=True)
    scaled = mixed * lax.rsqrt(square / (mixed.shape[0] * mixed.shape[1]) + EPS)
    normed = (scaled * gain_v[...]).astype(jnp.bfloat16)
    for p in range(n_groups):
        mine[p] = normed[p * sub : (p + 1) * sub]

    pl.semaphore_wait(barrier, n_section * count - 1)

    for step in order:
        if step:
            peer = partner(me, step, count)
            pltpu.make_async_remote_copy(
                src_ref=mine.at[lax.div(peer, n_rank)],
                dst_ref=gathered.at[me],
                send_sem=gather_sem.at[0],
                recv_sem=gather_sem.at[1],
                device_id=place(peer, section),
                device_id_type=MESH,
            ).start()
    mixed_copy = pltpu.make_async_remote_copy(
        src_ref=mixed_v,
        dst_ref=mixed_in,
        send_sem=mixed_sem.at[0],
        recv_sem=mixed_sem.at[1],
        device_id=place(me, after),
        device_id_type=MESH,
    )
    mixed_copy.start()
    gathered[me] = mine[group]

    others = gathered.at[pl.ds(0, count - 1)]
    pltpu.make_async_copy(others, others, gather_sem.at[1]).wait()
    for r in range(count):
        spread[r * sub : (r + 1) * sub] = gathered[r].astype(jnp.float32)
    block = jnp.concatenate(
        [spread[pl.ds(j, count, stride=sub), :] for j in range(sub)], axis=1
    ).astype(jnp.bfloat16)

    def piece_copy(p):
        at, size = pieces[p]
        return pltpu.make_async_remote_copy(
            src_ref=passing.at[:, pl.ds(at, size)],
            dst_ref=passed.at[:, pl.ds(at, size)],
            send_sem=piece_sem.at[0, p],
            recv_sem=piece_sem.at[1, p],
            device_id={"groups": 1 - group, "section": section, "rank": rank},
            device_id_type=MESH,
        )

    for copy in ups:
        copy.wait()
    for p, (at, size) in enumerate(pieces):
        total = 0.0
        for k in range(up_chunks):
            total = total + jnp.dot(
                block[:, k * depth : (k + 1) * depth],
                up_v[k, :, at : at + size],
                preferred_element_type=jnp.float32,
            )
        acc[:, at : at + size] = total
        passing[:, at : at + size] = total.astype(jnp.bfloat16)
        piece_copy(p).start()

    for p, (at, size) in enumerate(pieces):
        downs[p].wait()
        piece_copy(p).wait_recv()
        upward = acc[:, at : at + size] + passed[:, at : at + size].astype(jnp.float32)
        hidden = (upward / (1.0 + jnp.exp(-upward))).astype(jnp.bfloat16)
        for n in range(0, half, WIDTH):
            cols = slice(n, n + WIDTH)
            part = jnp.dot(
                hidden, down_v[at : at + size, cols], preferred_element_type=jnp.float32
            )
            lowered[:, cols] = lowered[:, cols] + part if p else part

    for j in range(sub):
        spread[pl.ds(j, count, stride=sub), :] = lowered[:, j * LANE : (j + 1) * LANE]
    for r in range(count):
        sending[r] = spread[r * sub : (r + 1) * sub].astype(jnp.bfloat16)
    for step in order:
        peer = partner(me, step, count)
        pltpu.make_async_remote_copy(
            src_ref=sending.at[peer],
            dst_ref=landed.at[me],
            send_sem=part_sem.at[0],
            recv_sem=part_sem.at[1],
            device_id=place(peer, after),
            device_id_type=MESH,
        ).start()

    mixed_copy.wait_recv()
    pltpu.make_async_copy(landed, landed, part_sem.at[1]).wait()
    for p in range(n_groups):
        rows = slice(p * sub, (p + 1) * sub)
        total = mixed_in[rows]
        for r in range(n_rank):
            total = total + landed[p * n_rank + r].astype(jnp.float32)
        out_ref[rows] = total

    mixed_copy.wait_send()
    for p in range(len(pieces)):
        piece_copy(p).wait_send()
    pltpu.make_async_copy(others, others, gather_sem.at[0]).wait()
    pltpu.make_async_copy(sending, sending, part_sem.at[0]).wait()


def fused(
    mesh_sizes, rows_in, query, key_cache, value_cache, key_new, value_new, lengths, norm_gain,
    w_up, w_down,
):
    n_groups, n_section, n_rank = mesh_sizes
    count = n_rank * n_groups
    d, slots, kv = rows_in.shape[-1], key_cache.shape[2], key_cache.shape[3]
    units = w_up.shape[2]
    heads, kvh, half = d // HD, kv // HD, d // n_groups
    depth, sub = half // UP_CHUNKS, half // LANE
    pieces = [(at, min(PIECE, units - at)) for at in range(0, units, PIECE)]
    f32, bf16 = jnp.float32, jnp.bfloat16
    anywhere = pl.BlockSpec(memory_space=pltpu.HBM)
    out = pl.pallas_call(
        functools.partial(layer_kernel, mesh_sizes, pieces),
        out_shape=jax.ShapeDtypeStruct((heads, HD), f32),
        in_specs=[anywhere] * 10,
        out_specs=pl.BlockSpec(memory_space=pltpu.VMEM),
        scratch_shapes=[
            pltpu.VMEM((heads, HD), f32),
            pltpu.VMEM((1, 1, d), bf16),
            pltpu.VMEM((slots, kv), bf16),
            pltpu.VMEM((slots, kv), bf16),
            pltpu.VMEM((1, 1, kv), bf16),
            pltpu.VMEM((1, 1, kv), bf16),
            pltpu.VMEM((heads, HD), f32),
            pltpu.VMEM((UP_CHUNKS, depth, units), bf16),
            pltpu.VMEM((units, half), bf16),
            pltpu.VMEM((heads, HD), f32),
            pltpu.VMEM((heads, HD), f32),
            pltpu.VMEM((n_groups, sub, LANE), bf16),
            pltpu.VMEM((count, sub, LANE), bf16),
            pltpu.VMEM((count * sub, LANE), f32),
            pltpu.VMEM((count, units), f32),
            pltpu.VMEM((count, units), bf16),
            pltpu.VMEM((count, units), bf16),
            pltpu.VMEM((count, half), f32),
            pltpu.VMEM((count, sub, LANE), bf16),
            pltpu.VMEM((count, sub, LANE), bf16),
            pltpu.SMEM((1, 1), jnp.int32),
            pltpu.SemaphoreType.DMA((8,)),
            pltpu.SemaphoreType.DMA((UP_CHUNKS,)),
            pltpu.SemaphoreType.DMA((len(pieces),)),
            pltpu.SemaphoreType.DMA((2,)),
            pltpu.SemaphoreType.DMA((2,)),
            pltpu.SemaphoreType.DMA((2, len(pieces))),
            pltpu.SemaphoreType.DMA((2,)),
        ],
        compiler_params=pltpu.CompilerParams(
            collective_id=0, has_side_effects=True, vmem_limit_bytes=64 * 1024 * 1024 - 65536
        ),
        name="layer",
    )(
        lengths,
        rows_in.reshape(heads, HD),
        query,
        key_cache,
        value_cache,
        key_new,
        value_new,
        norm_gain.reshape(heads, HD),
        w_up,
        w_down,
    )
    return out.reshape(1, 1, d)


def attend_plain(query, key_cache, value_cache, key_new, value_new, length):
    kv = key_cache.shape[1] // HD
    out = attend(
        query.reshape(-1, HD).astype(jnp.float32),
        key_cache,
        value_cache,
        key_new.reshape(kv, HD).astype(jnp.float32),
        value_new.reshape(kv, HD).astype(jnp.float32),
        length,
    )
    return out.reshape(-1)


def plain(
    rows_in, query, key_cache, value_cache, key_new, value_new, lengths, norm_gain, w_up, w_down
):
    section_rows = rows_in[0]
    local_rows = section_rows.shape[0]
    attended = jax.vmap(attend_plain)(
        query[0], key_cache[0], value_cache[0], key_new[0], value_new[0], lengths[0]
    )
    mixed = section_rows + attended
    scaled = mixed * lax.rsqrt(jnp.mean(mixed * mixed, axis=-1, keepdims=True) + EPS)
    normed = (scaled * norm_gain[0][None, :]).astype(jnp.bfloat16)
    upward = jnp.dot(
        lax.all_gather(normed, "rank", axis=0, tiled=True),
        w_up[0],
        preferred_element_type=jnp.float32,
    )
    hidden = jax.nn.silu(upward).astype(jnp.bfloat16)
    whole = lax.psum(jnp.dot(hidden, w_down[0], preferred_element_type=jnp.float32), "rank")
    mine = lax.dynamic_slice_in_dim(whole, lax.axis_index("rank") * local_rows, local_rows, 0)
    size = lax.axis_size("section")
    pairs = [(source, (source + 1) % size) for source in range(size)]
    return lax.ppermute(mixed + mine, "section", pairs)[None]


def solution(mesh):
    n_groups, n_section, n_rank = (mesh.shape[a] for a in ("groups", "section", "rank"))
    sizes = (n_groups, n_section, n_rank)
    count = n_groups * n_rank

    def per_device(*args):
        rows, d = args[0].shape[1], args[0].shape[2]
        units = args[8].shape[2]
        fits = (
            rows == 1
            and n_groups == 2
            and n_section > 1
            and count & (count - 1) == 0
            and count <= 32
            and units % LANE == 0
            and d % (16 * LANE * n_groups) == 0
            and d % (WIDTH * n_groups) == 0
            and d % (LANE * n_groups * UP_CHUNKS) == 0
            and 4 * d // n_groups * units < 60 * 1000 * 1000
        )
        if fits:
            return fused(sizes, *args)
        return plain(*args)

    placed = (
        P("section", ("groups", "rank"), None),
        P("section", ("groups", "rank"), None),
        P("section", ("groups", "rank"), None, None),
        P("section", ("groups", "rank"), None, None),
        P("section", ("groups", "rank"), None),
        P("section", ("groups", "rank"), None),
        P("section", ("groups", "rank")),
        P("section", None),
        P("section", None, "rank"),
        P("section", "rank", None),
    )
    return jax.shard_map(
        per_device,
        mesh=mesh,
        in_specs=placed,
        out_specs=P("section", ("groups", "rank"), None),
        check_vma=False,
    )
```

time: 28.5 us -> 27.4 us (0.961)
  Pallas kernels: 26.2 us -> 25.2 us
    pallas_call x1, Pallas kernels: 26.2 us -> 25.2 us  [fused(): pl.pallas_call(functools.partial(layer_kernel, mesh_sizes, pieces), out_s...]
where the time goes in v2:
time: 27.4 us; the launch traced here: 27.2 us
  Pallas kernels  25.2 us (92%)
  local copies, waits for them, and re-layouts  1.38 us (5%)
  between operations  0.66 us (2%)
    pallas_call x1, Pallas kernels, fused(): pl.pallas_call(functools.partial(layer_kernel, mesh_sizes, pieces), out_s...  25.2 us
    unnamed x1, local copies, waits for them, and re-layouts  1.38 us

profile of v2, /device:TPU:1, one launch (start us, length us, event | category | flops | bytes accessed | tf_op | source)
XLA Modules:
  0.0 27.2 jit_solution(14958494505010248721)
XLA Ops:
  0.7 25.2 %layer.1 = f32[64,128]{1,0:T(8,128)} custom-call(s32[1,1]{1,0:T(1,128)S(6)} %copy.12.len_in, f32[64,128]{1,0:T(8,128)} %bitcast.4, bf16[1,1,8192]{2,1,0:T(2,128)(2,1)} %q_ref.1, bf16[1,1,256,1024]{3,2,1,0:T(8,128)(2,1)} %kc_ref.1, bf16[1,1,256,1024]{3,2,1,0:T(8,128)(2,1)} %vc_ref.1, bf16[1,1,1024]{2,1,0:T(2,128)(2,1)} %kn_ref.1, bf16[1,1,1024]{2,1,0:T(2,128)(2,1)} %vn_ref.1, ...), custom_call_target="tpu_custom_call" | custom-call | tf_op jit(solution)/shard_map/layer/pallas_call | solution.py:272
  25.8 1.4 %copy.13 = f32[1,1,8192]{2,1,0:T(1,128)} copy(f32[1,1,8192]{2,1,0:T(1,128)} %bitcast.3) | data formatting | bytes 65536

commit v3 on v2

--- a/solution.py
+++ b/solution.py
@@ -13,6 +13,8 @@
 UP_CHUNKS = 4
 PIECE = 512
 WIDTH = 1024
+LEAD = 2
+SPLIT = 3
 MESH = pl.DeviceIdType.MESH
 
 
@@ -80,7 +82,7 @@
     out_ref,
     rows_v, q_v, kc_v, vc_v, kn_v, vn_v, gain_v, up_v, down_v,
     mixed_v, mixed_in, mine, gathered, spread, acc, passing, passed, lowered, sending, landed,
-    len_ref, small_sem, up_sem, down_sem, mixed_sem, gather_sem, piece_sem, part_sem,
+    len_ref, small_sem, up_sem, down_sem, mixed_sem, gather_sem, piece_sem, part_sem, turn,
 ):
     n_groups, n_section, n_rank = sizes
     count = n_rank * n_groups
@@ -88,6 +90,7 @@
     me = group * n_rank + rank
     after = lax.rem(section + 1, n_section)
     order = far_first(n_groups, n_rank)
+    root_first = sorted(range(count), key=lambda p: p % n_rank // 2 + p % 2 + p // n_rank)
     up_chunks, depth = up_v.shape[0], up_v.shape[1]
     half = up_chunks * depth
     sub = half // LANE
@@ -109,6 +112,21 @@
     ]
     for copy in small:
         copy.start()
+
+    ups = [
+        pltpu.make_async_copy(
+            up_ref.at[0, pl.ds(base + c * depth, depth)], up_v.at[c], up_sem.at[c]
+        )
+        for c in range(up_chunks)
+    ]
+    downs = [
+        pltpu.make_async_copy(
+            down_ref.at[0, pl.ds(at, size), pl.ds(base, half)],
+            down_v.at[pl.ds(at, size)],
+            down_sem.at[p],
+        )
+        for p, (at, size) in enumerate(pieces)
+    ]
 
     barrier = pltpu.get_barrier_semaphore()
     for step in order:
@@ -121,23 +139,8 @@
                     device_id_type=MESH,
                 )
 
-    ups = [
-        pltpu.make_async_copy(
-            up_ref.at[0, pl.ds(base + c * depth, depth)], up_v.at[c], up_sem.at[c]
-        )
-        for c in range(up_chunks)
-    ]
-    downs = [
-        pltpu.make_async_copy(
-            down_ref.at[0, pl.ds(at, size), pl.ds(base, half)],
-            down_v.at[pl.ds(at, size)],
-            down_sem.at[p],
-        )
-        for p, (at, size) in enumerate(pieces)
-    ]
-    for copy in ups + downs:
+    for copy in ups:
         copy.start()
-
     for copy in small:
         copy.wait()
     attended = attend(
@@ -158,17 +161,37 @@
 
     pl.semaphore_wait(barrier, n_section * count - 1)
 
-    for step in order:
-        if step:
-            peer = partner(me, step, count)
-            pltpu.make_async_remote_copy(
-                src_ref=mine.at[lax.div(peer, n_rank)],
-                dst_ref=gathered.at[me],
-                send_sem=gather_sem.at[0],
-                recv_sem=gather_sem.at[1],
-                device_id=place(peer, section),
-                device_id_type=MESH,
-            ).start()
+    def row_copy(peer, sem):
+        return pltpu.make_async_remote_copy(
+            src_ref=mine.at[lax.div(peer, n_rank)],
+            dst_ref=gathered.at[me],
+            send_sem=gather_sem.at[sem],
+            recv_sem=gather_sem.at[1],
+            device_id=place(peer, section),
+            device_id_type=MESH,
+        )
+
+    far = [step for step in order if step % n_rank >= n_rank // 2]
+    near = [step for step in order if step and step not in far]
+    lead = gathered.at[pl.ds(0, LEAD)]
+
+    @pl.when(section == 0)
+    def _():
+        for step in far[:LEAD]:
+            row_copy(partner(me, step, count), 0).start()
+        for step in far[LEAD:] + near:
+            row_copy(partner(me, step, count), 2).start()
+        pltpu.make_async_copy(lead, lead, gather_sem.at[0]).wait()
+        pl.semaphore_signal(turn, inc=1, device_id={"section": after}, device_id_type=MESH)
+
+    @pl.when(section != 0)
+    def _():
+        for step in far[:SPLIT] + near:
+            row_copy(partner(me, step, count), 2).start()
+        pl.semaphore_wait(turn, 1)
+        for step in far[SPLIT:]:
+            row_copy(partner(me, step, count), 2).start()
+
     mixed_copy = pltpu.make_async_remote_copy(
         src_ref=mixed_v,
         dst_ref=mixed_in,
@@ -179,6 +202,8 @@
     )
     mixed_copy.start()
     gathered[me] = mine[group]
+    for copy in downs:
+        copy.start()
 
     others = gathered.at[pl.ds(0, count - 1)]
     pltpu.make_async_copy(others, others, gather_sem.at[1]).wait()
@@ -229,8 +254,7 @@
         spread[pl.ds(j, count, stride=sub), :] = lowered[:, j * LANE : (j + 1) * LANE]
     for r in range(count):
         sending[r] = spread[r * sub : (r + 1) * sub].astype(jnp.bfloat16)
-    for step in order:
-        peer = partner(me, step, count)
+    for peer in root_first:
         pltpu.make_async_remote_copy(
             src_ref=sending.at[peer],
             dst_ref=landed.at[me],
@@ -252,7 +276,15 @@
     mixed_copy.wait_send()
     for p in range(len(pieces)):
         piece_copy(p).wait_send()
-    pltpu.make_async_copy(others, others, gather_sem.at[0]).wait()
+    @pl.when(section == 0)
+    def _():
+        rest = gathered.at[pl.ds(0, count - 1 - LEAD)]
+        pltpu.make_async_copy(rest, rest, gather_sem.at[2]).wait()
+
+    @pl.when(section != 0)
+    def _():
+        pltpu.make_async_copy(others, others, gather_sem.at[2]).wait()
+
     pltpu.make_async_copy(sending, sending, part_sem.at[0]).wait()
 
 
@@ -300,9 +332,10 @@
             pltpu.SemaphoreType.DMA((UP_CHUNKS,)),
             pltpu.SemaphoreType.DMA((len(pieces),)),
             pltpu.SemaphoreType.DMA((2,)),
-            pltpu.SemaphoreType.DMA((2,)),
+            pltpu.SemaphoreType.DMA((3,)),
             pltpu.SemaphoreType.DMA((2, len(pieces))),
             pltpu.SemaphoreType.DMA((2,)),
+            pltpu.SemaphoreType.REGULAR,
         ],
         compiler_params=pltpu.CompilerParams(
             collective_id=0, has_side_effects=True, vmem_limit_bytes=64 * 1024 * 1024 - 65536
@@ -371,7 +404,8 @@
         fits = (
             rows == 1
             and n_groups == 2
-            and n_section > 1
+            and n_section == 2
+            and n_rank >= 8
             and count & (count - 1) == 0
             and count <= 32
             and units % LANE == 0

time: 27.4 us -> 25.8 us (0.942)
  Pallas kernels: 25.2 us -> 23.5 us
    pallas_call x1, Pallas kernels: 25.2 us -> 23.5 us  [fused(): pl.pallas_call(functools.partial(layer_kernel, mesh_sizes, pieces), out_s...]
where the time goes in v3:
time: 25.8 us; the launch traced here: 25.6 us
  Pallas kernels  23.5 us (91%)
  local copies, waits for them, and re-layouts  1.38 us (5%)
  between operations  0.66 us (3%)
    pallas_call x1, Pallas kernels, fused(): pl.pallas_call(functools.partial(layer_kernel, mesh_sizes, pieces), out_s...  23.5 us
    unnamed x1, local copies, waits for them, and re-layouts  1.38 us

profile of v3, /device:TPU:1, one launch (start us, length us, event | category | flops | bytes accessed | tf_op | source)
XLA Modules:
  0.0 25.6 jit_solution(17940005477116187477)
XLA Ops:
  0.7 23.5 %layer.1 = f32[64,128]{1,0:T(8,128)} custom-call(s32[1,1]{1,0:T(1,128)S(6)} %copy.12.len_in, f32[64,128]{1,0:T(8,128)} %bitcast.4, bf16[1,1,8192]{2,1,0:T(2,128)(2,1)} %q_ref.1, bf16[1,1,256,1024]{3,2,1,0:T(8,128)(2,1)} %kc_ref.1, bf16[1,1,256,1024]{3,2,1,0:T(8,128)(2,1)} %vc_ref.1, bf16[1,1,1024]{2,1,0:T(2,128)(2,1)} %kn_ref.1, bf16[1,1,1024]{2,1,0:T(2,128)(2,1)} %vn_ref.1, ...), custom_call_target="tpu_custom_call" | custom-call | tf_op jit(solution)/shard_map/layer/pallas_call | solution.py:304
  24.2 1.4 %copy.13 = f32[1,1,8192]{2,1,0:T(1,128)} copy(f32[1,1,8192]{2,1,0:T(1,128)} %bitcast.3) | data formatting | bytes 65536

commit v4 on v3

--- a/solution.py
+++ b/solution.py
@@ -11,7 +11,7 @@
 EPS = 1e-05
 LANE = 128
 UP_CHUNKS = 4
-PIECE = 512
+PIECE = 1024
 WIDTH = 1024
 LEAD = 2
 SPLIT = 3
@@ -159,6 +159,7 @@
     for p in range(n_groups):
         mine[p] = normed[p * sub : (p + 1) * sub]
 
+    gathered[me] = mine[group]
     pl.semaphore_wait(barrier, n_section * count - 1)
 
     def row_copy(peer, sem):
@@ -201,11 +202,12 @@
         device_id_type=MESH,
     )
     mixed_copy.start()
-    gathered[me] = mine[group]
     for copy in downs:
         copy.start()
 
     others = gathered.at[pl.ds(0, count - 1)]
+    for copy in ups:
+        copy.wait()
     pltpu.make_async_copy(others, others, gather_sem.at[1]).wait()
     for r in range(count):
         spread[r * sub : (r + 1) * sub] = gathered[r].astype(jnp.float32)
@@ -218,14 +220,12 @@
         return pltpu.make_async_remote_copy(
             src_ref=passing.at[:, pl.ds(at, size)],
             dst_ref=passed.at[:, pl.ds(at, size)],
-            send_sem=piece_sem.at[0, p],
-            recv_sem=piece_sem.at[1, p],
+            send_sem=piece_sem.at[len(pieces)],
+            recv_sem=piece_sem.at[p],
             device_id={"groups": 1 - group, "section": section, "rank": rank},
             device_id_type=MESH,
         )
 
-    for copy in ups:
-        copy.wait()
     for p, (at, size) in enumerate(pieces):
         total = 0.0
         for k in range(up_chunks):
@@ -248,21 +248,29 @@
             part = jnp.dot(
                 hidden, down_v[at : at + size, cols], preferred_element_type=jnp.float32
             )
-            lowered[:, cols] = lowered[:, cols] + part if p else part
-
-    for j in range(sub):
-        spread[pl.ds(j, count, stride=sub), :] = lowered[:, j * LANE : (j + 1) * LANE]
-    for r in range(count):
-        sending[r] = spread[r * sub : (r + 1) * sub].astype(jnp.bfloat16)
-    for peer in root_first:
-        pltpu.make_async_remote_copy(
+            total = lowered[:, cols] + part if p else part
+            if p < len(pieces) - 1:
+                lowered[:, cols] = total
+            else:
+                for j in range(WIDTH // LANE):
+                    h = n // LANE + j
+                    spread[h * count : (h + 1) * count] = total[:, j * LANE : (j + 1) * LANE]
+
+    def part_copy(peer):
+        return pltpu.make_async_remote_copy(
             src_ref=sending.at[peer],
             dst_ref=landed.at[me],
             send_sem=part_sem.at[0],
             recv_sem=part_sem.at[1],
             device_id=place(peer, after),
             device_id_type=MESH,
-        ).start()
+        )
+
+    for i, peer in enumerate(root_first):
+        sending[peer] = spread[pl.ds(peer, sub, stride=count), :].astype(jnp.bfloat16)
+        if i:
+            part_copy(root_first[i - 1]).start()
+    part_copy(root_first[-1]).start()
 
     mixed_copy.wait_recv()
     pltpu.make_async_copy(landed, landed, part_sem.at[1]).wait()
@@ -274,8 +282,7 @@
         out_ref[rows] = total
 
     mixed_copy.wait_send()
-    for p in range(len(pieces)):
-        piece_copy(p).wait_send()
+    pltpu.make_async_copy(passing, passing, piece_sem.at[len(pieces)]).wait()
     @pl.when(section == 0)
     def _():
         rest = gathered.at[pl.ds(0, count - 1 - LEAD)]
@@ -333,7 +340,7 @@
             pltpu.SemaphoreType.DMA((len(pieces),)),
             pltpu.SemaphoreType.DMA((2,)),
             pltpu.SemaphoreType.DMA((3,)),
-            pltpu.SemaphoreType.DMA((2, len(pieces))),
+            pltpu.SemaphoreType.DMA((len(pieces) + 1,)),
             pltpu.SemaphoreType.DMA((2,)),
             pltpu.SemaphoreType.REGULAR,
         ],

time: 25.8 us -> 25.2 us (0.977)
  Pallas kernels: 23.5 us -> 23 us
    pallas_call x1, Pallas kernels: 23.5 us -> 23 us  [fused(): pl.pallas_call(functools.partial(layer_kernel, mesh_sizes, pieces), out_s...]
where the time goes in v4:
time: 25.2 us; the launch traced here: 25 us
  Pallas kernels  23 us (91%)
  local copies, waits for them, and re-layouts  1.38 us (5%)
  between operations  0.66 us (3%)
    pallas_call x1, Pallas kernels, fused(): pl.pallas_call(functools.partial(layer_kernel, mesh_sizes, pieces), out_s...  23 us
    unnamed x1, local copies, waits for them, and re-layouts  1.38 us

profile of v4, /device:TPU:1, one launch (start us, length us, event | category | flops | bytes accessed | tf_op | source)
XLA Modules:
  0.0 25.0 jit_solution(7900857145208850192)
XLA Ops:
  0.7 23.0 %layer.1 = f32[64,128]{1,0:T(8,128)} custom-call(s32[1,1]{1,0:T(1,128)S(6)} %copy.12.len_in, f32[64,128]{1,0:T(8,128)} %bitcast.4, bf16[1,1,8192]{2,1,0:T(2,128)(2,1)} %q_ref.1, bf16[1,1,256,1024]{3,2,1,0:T(8,128)(2,1)} %kc_ref.1, bf16[1,1,256,1024]{3,2,1,0:T(8,128)(2,1)} %vc_ref.1, bf16[1,1,1024]{2,1,0:T(2,128)(2,1)} %kn_ref.1, bf16[1,1,1024]{2,1,0:T(2,128)(2,1)} %vn_ref.1, ...), custom_call_target="tpu_custom_call" | custom-call | tf_op jit(solution)/shard_map/layer/pallas_call | solution.py:311
  23.6 1.4 %copy.13 = f32[1,1,8192]{2,1,0:T(1,128)} copy(f32[1,1,8192]{2,1,0:T(1,128)} %bitcast.3) | data formatting | bytes 65536

commit v5 on v4

--- a/solution.py
+++ b/solution.py
@@ -13,7 +13,7 @@
 UP_CHUNKS = 4
 PIECE = 1024
 WIDTH = 1024
-LEAD = 2
+LEAD = 3
 SPLIT = 3
 MESH = pl.DeviceIdType.MESH
 
@@ -172,26 +172,36 @@
             device_id_type=MESH,
         )
 
-    far = [step for step in order if step % n_rank >= n_rank // 2]
-    near = [step for step in order if step and step not in far]
+    half_rank = n_rank // 2
+    high = lax.div(rank, half_rank)
+    far = []
+    for z in range(half_rank // 2):
+        for step in (3, 2, 1, 0):
+            end = 2 * (half_rank - 1 - z) * (1 - high) + 2 * z * high
+            side = lax.rem(rank, 2) if step % 2 == 0 else 1 - lax.rem(rank, 2)
+            team = group if step < 2 else 1 - group
+            far.append(team * n_rank + end + side)
+    near = [
+        partner(me, step, count) for step in order if step and step % n_rank < half_rank
+    ]
     lead = gathered.at[pl.ds(0, LEAD)]
 
     @pl.when(section == 0)
     def _():
-        for step in far[:LEAD]:
-            row_copy(partner(me, step, count), 0).start()
-        for step in far[LEAD:] + near:
-            row_copy(partner(me, step, count), 2).start()
+        for peer in far[:LEAD]:
+            row_copy(peer, 0).start()
+        for peer in far[LEAD:] + near:
+            row_copy(peer, 2).start()
         pltpu.make_async_copy(lead, lead, gather_sem.at[0]).wait()
         pl.semaphore_signal(turn, inc=1, device_id={"section": after}, device_id_type=MESH)
 
     @pl.when(section != 0)
     def _():
-        for step in far[:SPLIT] + near:
-            row_copy(partner(me, step, count), 2).start()
+        for peer in far[:SPLIT] + near:
+            row_copy(peer, 2).start()
         pl.semaphore_wait(turn, 1)
-        for step in far[SPLIT:]:
-            row_copy(partner(me, step, count), 2).start()
+        for peer in far[SPLIT:]:
+            row_copy(peer, 2).start()
 
     mixed_copy = pltpu.make_async_remote_copy(
         src_ref=mixed_v,

time: 25.2 us -> 24.9 us (0.988)
  Pallas kernels: 23 us -> 22.6 us
    pallas_call x1, Pallas kernels: 23 us -> 22.6 us  [fused(): pl.pallas_call(functools.partial(layer_kernel, mesh_sizes, pieces), out_s...]
where the time goes in v5:
time: 24.9 us; the launch traced here: 24.7 us
  Pallas kernels  22.6 us (91%)
  local copies, waits for them, and re-layouts  1.38 us (6%)
  between operations  0.66 us (3%)
    pallas_call x1, Pallas kernels, fused(): pl.pallas_call(functools.partial(layer_kernel, mesh_sizes, pieces), out_s...  22.6 us
    unnamed x1, local copies, waits for them, and re-layouts  1.38 us

profile of v5, /device:TPU:1, one launch (start us, length us, event | category | flops | bytes accessed | tf_op | source)
XLA Modules:
  0.0 24.7 jit_solution(812206310637922841)
XLA Ops:
  0.7 22.6 %layer.1 = f32[64,128]{1,0:T(8,128)} custom-call(s32[1,1]{1,0:T(1,128)S(6)} %copy.12.len_in, f32[64,128]{1,0:T(8,128)} %bitcast.4, bf16[1,1,8192]{2,1,0:T(2,128)(2,1)} %q_ref.1, bf16[1,1,256,1024]{3,2,1,0:T(8,128)(2,1)} %kc_ref.1, bf16[1,1,256,1024]{3,2,1,0:T(8,128)(2,1)} %vc_ref.1, bf16[1,1,1024]{2,1,0:T(2,128)(2,1)} %kn_ref.1, bf16[1,1,1024]{2,1,0:T(2,128)(2,1)} %vn_ref.1, ...), custom_call_target="tpu_custom_call" | custom-call | tf_op jit(solution)/shard_map/layer/pallas_call | solution.py:321
  23.3 1.4 %copy.13 = f32[1,1,8192]{2,1,0:T(1,128)} copy(f32[1,1,8192]{2,1,0:T(1,128)} %bitcast.3) | data formatting | bytes 65536
